TPU v7x, 32 devices: a whole 2x2x4 slice. The times are simulated.
32 devices in a mesh: dp: 32 (over z, y, x, core).
Axes of the slice: x: 2, y: 2, z: 4, core: 2. Of those that a mesh axis runs over, the one named last changes fastest.
Arguments:
- features: bfloat16 [32768, 3136], P('dp'), may hold values from -6 to 6
- w_one: bfloat16 [512, 3136], replicated, may hold values from -0.109375 to 0.109375
- b_one: float32 [512], replicated, may hold values from -3 to 3
- w_two: bfloat16 [512, 918], replicated, may hold values from -0.25 to 0.25
- b_two: float32 [918], replicated, may hold values from -112 to 112
- action: int32 [32768], P('dp'), may hold values from 0 to 17
- target_probs: float32 [32768, 18, 51], P('dp'), may hold values from 0 to 1, as said below
- next_action: int32 [32768], P('dp'), may hold values from 0 to 17
- lower_idx: int32 [32768, 51], P('dp'), may hold values from 0 to 49
- upper_frac: float32 [32768, 51], P('dp'), may hold values from 0 to 1
- is_weight: float32 [32768], P('dp'), may hold values from 0.1 to 1
Outputs:
- grad_w1: float32 [512, 3136], replicated
- grad_b1: float32 [512], replicated
- grad_w2: float32 [512, 918], replicated
- grad_b2: float32 [918], replicated
- mean_loss: float32 [], replicated
- priorities: float32 [32768], P('dp')
Inputs may be any that keep to these rules, and one draw needn't show every extreme that they name: Each target_probs[i, a] is a distribution over the atoms: positive entries that sum to one.
All inputs are finite; a program needn't handle non-finite values.
Results may differ from a plain program's by a relative error of at most 0.005.
Values sent between devices are 32-bit elements; how exact they have to be, the bound alone decides.
A program may use at most 128 MiB of HBM per device.

v0:
```python
import jax
import jax.numpy as jnp
from jax import lax
from jax.sharding import PartitionSpec as P


def forward_loss(
    features,
    w_one,
    b_one,
    w_two,
    b_two,
    action,
    target_probs,
    next_action,
    lower_idx,
    upper_frac,
    is_weight,
):
    row_count = features.shape[0]
    n_act = target_probs.shape[1]
    n_atom = target_probs.shape[2]
    pre_act = (
        lax.dot_general(
            features, w_one, (((1,), (1,)), ((), ())), preferred_element_type=jnp.float32
        )
        + b_one
    )
    hidden = jnp.maximum(pre_act, 0.0).astype(jnp.bfloat16)
    logits = (jnp.dot(hidden, w_two, preferred_element_type=jnp.float32) + b_two).reshape(
        row_count, n_act, n_atom
    )
    chosen = jnp.take_along_axis(logits, action[:, None, None], axis=1)[:, 0, :]
    log_probs = jax.nn.log_softmax(chosen, axis=-1)
    next_probs = jnp.take_along_axis(target_probs, next_action[:, None, None], axis=1)[:, 0, :]
    atom_ids = jnp.arange(n_atom, dtype=jnp.int32)
    mass_low = next_probs * (1.0 - upper_frac)
    mass_high = next_probs * upper_frac
    low_hot = lower_idx[:, :, None] == atom_ids[None, None, :]
    high_hot = lower_idx[:, :, None] + 1 == atom_ids[None, None, :]
    projected = jnp.sum(
        jnp.where(low_hot, mass_low[:, :, None], 0.0)
        + jnp.where(high_hot, mass_high[:, :, None], 0.0),
        axis=1,
    )
    cross_ent = -jnp.sum(projected * log_probs, axis=-1)
    grad_chosen = is_weight[:, None] * (
        jnp.exp(log_probs) * jnp.sum(projected, axis=-1, keepdims=True) - projected
    )
    act_hot = action[:, None] == jnp.arange(n_act, dtype=jnp.int32)[None, :]
    grad_logits = (
        jnp.where(act_hot[:, :, None], grad_chosen[:, None, :], 0.0)
        .reshape(row_count, n_act * n_atom)
        .astype(jnp.bfloat16)
    )
    grad_hidden = lax.dot_general(
        grad_logits, w_two, (((1,), (1,)), ((), ())), preferred_element_type=jnp.float32
    )
    grad_pre = jnp.where(pre_act > 0.0, grad_hidden, 0.0).astype(jnp.bfloat16)
    return (hidden, grad_logits, grad_pre, cross_ent)


def on_device(
    features,
    w_one,
    b_one,
    w_two,
    b_two,
    action,
    target_probs,
    next_action,
    lower_idx,
    upper_frac,
    is_weight,
):
    total_rows = features.shape[0] * lax.axis_size("dp")
    hidden, grad_logits, grad_pre, cross_ent = forward_loss(
        features,
        w_one,
        b_one,
        w_two,
        b_two,
        action,
        target_probs,
        next_action,
        lower_idx,
        upper_frac,
        is_weight,
    )
    local_loss = jnp.sum(is_weight * cross_ent)
    local_top = jnp.max(cross_ent)
    loss_sum = lax.psum(local_loss, "dp")
    top = lax.pmax(local_top, "dp")
    local_w2 = lax.dot_general(
        hidden, grad_logits, (((0,), (0,)), ((), ())), preferred_element_type=jnp.float32
    )
    local_b2 = jnp.sum(grad_logits.astype(jnp.float32), axis=0)
    local_b1 = jnp.sum(grad_pre.astype(jnp.float32), axis=0)
    grad_b1, grad_w2, grad_b2 = lax.psum((local_b1, local_w2, local_b2), "dp")
    local_w1 = lax.dot_general(
        grad_pre, features, (((0,), (0,)), ((), ())), preferred_element_type=jnp.float32
    )
    grad_w1 = lax.psum(local_w1, "dp")
    priorities = cross_ent / jnp.maximum(top, 1.0)
    mean_loss = loss_sum / total_rows
    return (grad_w1, grad_b1, grad_w2, grad_b2, mean_loss, priorities)


def solution(mesh):
    in_specs = (
        P("dp", None),
        P(),
        P(),
        P(),
        P(),
        P("dp"),
        P("dp", None, None),
        P("dp"),
        P("dp", None),
        P("dp", None),
        P("dp"),
    )
    out_specs = (P(), P(), P(), P(), P(), P("dp"))
    return jax.shard_map(
        on_device, mesh=mesh, in_specs=in_specs, out_specs=out_specs, check_vma=False
    )
```

profile of v0, /device:TPU:1, one launch (start us, length us, event | category | flops | bytes accessed | tf_op | source)
XLA Modules:
  0.0 283.0 jit_solution(31237595956415352)
XLA Ops:
  7.2 0.9 and_reduce_fusion
  8.1 0.8 iota_compare_fusion.2
  8.9 0.7 and_reduce_fusion.1
  9.6 1.0 broadcast_add_fusion
  10.6 5.9 %fusion.16 = f32[1024,512]{1,0:T(8,128)S(1)} fusion(bf16[1024,3136]{0,1:T(8,128)(2,1)} %param.13, bf16[512,3136]{0,1:T(8,128)(2,1)S(1)} %copy-done), kind=kOutput, calls=%fused_computation.50 | convolution fusion | flops 3288334336 | bytes 11730944 | tf_op jit(solution)/shard_map/dot_general | solution.py:24
  16.5 1.3 copy-done.10
  17.8 3.0 %convolution_add_fusion = f32[1024,918]{0,1:T(8,128)} fusion(bf16[512,918]{0,1:T(8,128)(2,1)S(1)} %copy-done.7, f32[918]{0:T(1024)S(1)} %copy-done.8, f32[1024,512]{1,0:T(8,128)S(1)} %fusion.16, f32[512]{0:T(512)S(1)} %copy-done.9), kind=kOutput, calls=%fused_computation.12 | convolution fusion | flops 965105664 | bytes 6803032 | tf_op jit(solution)/shard_map/dot_general | solution.py:30
  20.8 3.9 %reshape.118 = f32[1024,18,51]{0,2,1:T(8,128)} reshape(f32[1024,918]{0,1:T(8,128)} %convolution_add_fusion) | data formatting | bytes 7520256 | tf_op jit(solution)/shard_map/reshape | solution.py:30
  24.7 7.5 %copy.39 = f32[1024,18,51]{2,0,1:T(8,128)} copy(f32[1024,18,51]{0,2,1:T(8,128)} %reshape.118) | data formatting | bytes 7520256 | tf_op jit(solution)/shard_map/reshape | solution.py:30
  32.2 10.5 %gather_fusion = f32[1024,51]{1,0:T(8,128)S(1)} fusion(f32[1024,18,51]{2,0,1:T(8,128)} %copy.39, s32[1024]{0:T(1024)S(1)} %bitcast.54), kind=kCustom, calls=%fused_computation.clone | custom fusion | bytes 425984 | tf_op jit(solution)/shard_map/jit(take_along_axis)/gather | solution.py:33
  43.6 7.5 %copy.40 = f32[1024,18,51]{2,0,1:T(8,128)} copy(f32[1024,18,51]{0,2,1:T(8,128)} %param.19) | data formatting | bytes 7520256 | tf_op args[6]
  51.1 10.6 %gather_fusion.1 = f32[1024,51]{1,0:T(8,128)S(1)} fusion(f32[1024,18,51]{2,0,1:T(8,128)} %copy.40, s32[1024]{0:T(1024)S(1)} %bitcast.53), kind=kCustom, calls=%fused_computation.1.clone | custom fusion | bytes 425984 | tf_op jit(solution)/shard_map/jit(take_along_axis)/gather | solution.py:35
  62.0 4.5 %fusion.1 = (f32[1024]{0:T(1024)S(1)}, f32[1024,51]{0,1:T(8,128)S(1)}) fusion(f32[1024,51]{0,1:T(8,128)S(1)} %get-tuple-element.21, s32[1024,51]{0,1:T(8,128)S(1)} %broadcast_add_fusion, f32[1024,51]{0,1:T(8,128)S(1)} %get-tuple-element.20, s32[1024,51]{0,1:T(8,128)S(1)} %copy-done.4), kind=kLoop, calls=%fused_computation.5 | loop fusion | flops 18590720 | bytes 1048576 | tf_op jit(solution)/shard_map/reduce_sum | solution.py:48
  66.7 1.1 fusion.3
  68.3 1.8 convert_element_type.22
  70.1 3.9 %convert_reduce_fusion.1 = (f32[512]{0:T(512)S(1)}, bf16[1024,512]{1,0:T(8,128)(2,1)S(1)}) fusion(bf16[1024,918]{0,1:T(8,128)(2,1)} %convert_element_type.22, bf16[512,918]{0,1:T(8,128)(2,1)} %param.16, f32[1024,512]{1,0:T(8,128)} %copy-done.10, f32[512]{0:T(512)S(1)} %copy-done.9), kind=kOutput, calls=%fused_computation.9 | convolution fusion | flops 965737984 | bytes 5969920 | tf_op jit(solution)/shard_map/dot_general | solution.py:56
  74.1 2.4 fusion.5
  76.5 8.2 %fusion.17 = f32[512,3136]{0,1:T(8,128)} fusion(bf16[1024,3136]{0,1:T(8,128)(2,1)} %param.13, bf16[1024,512]{1,0:T(8,128)(2,1)S(1)} %get-tuple-element.25), kind=kOutput, calls=%fused_computation.51 | convolution fusion | flops 3288334336 | bytes 13893632 | tf_op jit(solution)/shard_map/dot_general | solution.py:100
  84.7 0.6 multiply_reduce_fusion
  85.9 43.3 %pmax.7 = f32[]{:T(128)} all-reduce(f32[]{:T(128)} %get-tuple-element.9), channel_id=1, replica_groups=mesh['dp'=32] {'dp'}, use_global_device_ids=true, to_apply=%region_14.16 | all-reduce | flops 1 | bytes 8 | tf_op jit(solution)/shard_map/pmax | solution.py:93
  130.4 41.3 %all-reduce = (f32[512]{0:T(512)}, f32[918]{0:T(1024)}, f32[]{:T(128)}) all-reduce(f32[512]{0:T(512)S(1)} %get-tuple-element.24, f32[918]{0:T(1024)S(1)} %reduce_sum.74, f32[]{:T(128)} %get-tuple-element.10), channel_id=1, replica_groups=mesh['dp'=32] {'dp'}, use_global_device_ids=true, to_apply=%region_6.8 | all-reduce | flops 1431 | bytes 11448 | tf_op jit(solution)/shard_map/psum | solution.py:99
  173.0 94.3 %all-reduce.4.cloned.1.call-done = (f32[512,3136]{0,1:T(8,128)}, f32[512,918]{0,1:T(8,128)}) async-done(((f32[512,3136]{0,1:T(8,128)}, f32[512,918]{0,1:T(8,128)}), (f32[512,3136]{0,1:T(8,128)}, f32[512,918]{0,1:T(8,128)})) %all-reduce.4.cloned.1.call-update) | async-done | bytes 8302608 | tf_op jit(solution)/shard_map/psum | solution.py:103
  267.2 6.5 %copy.47 = f32[512,3136]{0,1:T(8,128)} copy(f32[512,3136]{0,1:T(8,128)} %get-tuple-element.28) | data formatting | bytes 12845056
  273.7 1.2 copy.48
  (40 shorter events, 3.8 us)
Async XLA Ops:
  7.2 3.4 %copy-start = (bf16[512,3136]{0,1:T(8,128)(2,1)S(1)}, bf16[512,3136]{0,1:T(8,128)(2,1)}, u32[]{:S(2)}) copy-start(bf16[512,3136]{0,1:T(8,128)(2,1)} %param.14) | copy-start | bytes 9633796
  7.2 260.1 %all-reduce.4.cloned.1.call-start = ((), (), s32[]{:S(2)}) async-start(), calls=%async_computation | async-start | bytes 16613376 | tf_op jit(solution)/shard_map/psum | solution.py:103
  10.5 7.3 %copy-start.7 = (bf16[512,918]{0,1:T(8,128)(2,1)S(1)}, bf16[512,918]{0,1:T(8,128)(2,1)}, u32[]{:S(2)}) copy-start(bf16[512,918]{0,1:T(8,128)(2,1)} %param.16) | copy-start | bytes 2820100
  10.6 7.3 %copy-start.8 = (f32[918]{0:T(1024)S(1)}, f32[918]{0:T(1024)}, u32[]{:S(2)}) copy-start(f32[918]{0:T(1024)} %param.17) | copy-start | bytes 11020
  10.6 7.2 %copy-start.9 = (f32[512]{0:T(512)S(1)}, f32[512]{0:T(512)}, u32[]{:S(2)}) copy-start(f32[512]{0:T(512)} %param.15) | copy-start | bytes 6148
  16.5 1.3 copy-start.10
  51.1 10.8 %copy-start.5 = (f32[1024,51]{0,1:T(8,128)S(1)}, f32[1024,51]{0,1:T(8,128)}, u32[]{:S(2)}) copy-start(f32[1024,51]{0,1:T(8,128)} %param.22) | copy-start | bytes 626692
  51.1 10.9 %copy-start.4 = (s32[1024,51]{0,1:T(8,128)S(1)}, s32[1024,51]{0,1:T(8,128)}, u32[]{:S(2)}) copy-start(s32[1024,51]{0,1:T(8,128)} %param.21) | copy-start | bytes 626692
  61.7 5.0 %copy-start.6 = (f32[1024]{0:T(1024)S(1)}, f32[1024]{0:T(1024)}, u32[]{:S(2)}) copy-start(f32[1024]{0:T(1024)} %param.23) | copy-start | bytes 12292
  70.1 3.9 %copy-start.3 = (bf16[1024,918]{0,1:T(8,128)(2,1)S(1)}, bf16[1024,918]{0,1:T(8,128)(2,1)}, u32[]{:S(2)}) copy-start(bf16[1024,918]{0,1:T(8,128)(2,1)} %convert_element_type.22) | copy-start | bytes 5640196
  70.1 3.9 %copy-start.11 = (f32[1024,512]{1,0:T(8,128)S(1)}, f32[1024,512]{1,0:T(8,128)}, u32[]{:S(2)}) copy-start(f32[1024,512]{1,0:T(8,128)} %copy-done.10) | copy-start | bytes 6291460
  267.2 6.5 %copy-start.2 = (f32[512,918]{0,1:T(8,128)S(1)}, f32[512,918]{0,1:T(8,128)}, u32[]{:S(2)}) copy-start(f32[512,918]{0,1:T(8,128)} %get-tuple-element.30) | copy-start | bytes 5640196
  267.2 7.7 %copy-start.1 = (bf16[512,3136]{0,1:T(8,128)(2,1)S(1)}, bf16[512,3136]{0,1:T(8,128)(2,1)}, u32[]{:S(2)}) copy-start(bf16[512,3136]{0,1:T(8,128)(2,1)} %param.14) | copy-start | bytes 9633796
Sparse Core Ops, SparseCore 0:
  84.8 182.3 all-reduce.3
where the time goes:
time: 284 us; the launch traced here: 283 us
  waiting for transfers between devices  94.3 us (33%)
  blocking collectives  84.6 us (30%)
  local copies, waits for them, and re-layouts  51.4 us (18%)
  matrix products  23.4 us (8%)
  between operations  16.7 us (6%)
  other arithmetic  12.5 us (4%)
    psum x1, waiting for transfers between devices, on_device(): grad_w1 = lax.psum(local_w1, 'dp')  94.3 us
    pmax x1, blocking collectives, on_device(): top = lax.pmax(local_top, 'dp')  43.3 us
    psum x1, blocking collectives, on_device(): grad_b1, grad_w2, grad_b2 = lax.psum((local_b1, local_w2, local_b2), 'dp')  41.3 us
    unnamed x27, local copies, waits for them, and re-layouts  16.6 us
    reshape x2, local copies, waits for them, and re-layouts, forward_loss(): (jnp.dot(hidden, w_two, preferred_element_type=jnp.float32) + b_two).resh...  11.3 us
    gather x2, local copies, waits for them, and re-layouts, forward_loss(): jnp.take_along_axis(target_probs, next_action[:, None, None], axis=1)  10.8 us
    gather x1, local copies, waits for them, and re-layouts, forward_loss(): chosen = jnp.take_along_axis(logits, action[:, None, None], axis=1)[:, 0, :]  10.5 us
    dot_general x1, matrix products, on_device(): lax.dot_general(grad_pre, features, (((0,), (0,)), ((), ())), preferred_e...  8.19 us
  transfers between devices with their start and end apart: 1, of which 1 were waited for; matrix products, arithmetic and copies ran while one was open for 1% of the time, Pallas kernels for 0%

commit v1 on v0

v1 whole, which is shorter than its diff:
```python
import functools

import jax
import jax.numpy as jnp
from jax import lax
from jax.experimental import pallas as pl
from jax.experimental.pallas import tpu as pltpu
from jax.sharding import PartitionSpec as P

MESH = pl.DeviceIdType.MESH
F32 = jnp.float32
BF16 = jnp.bfloat16
VMEM_LIMIT = 60 * 1024 * 1024


def pad_up(value, step):
    return -(-value // step) * step


def dot(a, b, ca, cb):
    return lax.dot_general(a, b, (((ca,), (cb,)), ((), ())), preferred_element_type=F32)


def head_kernel(
    n_act, n_atom, slot,
    pre_ref, w2_ref, b2_ref, act_ref, tp_ref, nxt_ref, low_ref, frac_ref, wgt_ref,
    gp_ref, gw2_ref, gb1_ref, gb2_ref, ce_ref, acc_ref,
):
    step = pl.program_id(0)
    last = pl.num_programs(0) - 1
    pre = pre_ref[...]
    cols = pre.shape[1]
    hidden = jnp.maximum(pre, 0.0).astype(BF16)
    logits = dot(w2_ref[...], hidden, 1, 0) + b2_ref[...]
    act = act_ref[...]
    nxt = nxt_ref[...]
    chosen = jnp.zeros((slot, cols), F32)
    for a in range(n_act):
        chosen = jnp.where(act == a, logits[a * slot:(a + 1) * slot], chosen)
    atom = lax.broadcasted_iota(jnp.int32, (slot, cols), 0)
    real = atom < n_atom
    chosen = jnp.where(real, chosen, -jnp.inf)
    shifted = chosen - jnp.max(chosen, axis=0, keepdims=True)
    log_z = jnp.log(jnp.sum(jnp.exp(shifted), axis=0, keepdims=True))
    log_probs = jnp.where(real, shifted - log_z, 0.0)
    probs = jnp.where(real, jnp.exp(log_probs), 0.0)
    nprob = jnp.zeros((n_atom, cols), F32)
    for a in range(n_act):
        nprob = jnp.where(nxt == a, tp_ref[a], nprob)
    frac = frac_ref[...]
    mass_low = nprob * (1.0 - frac)
    mass_high = nprob * frac
    low = low_ref[...]
    proj = jnp.zeros((slot, cols), F32)
    for j in range(n_atom):
        dist = atom - low[j:j + 1]
        proj = proj + jnp.where(
            dist == 0, mass_low[j:j + 1], jnp.where(dist == 1, mass_high[j:j + 1], 0.0)
        )
    ce_ref[...] = -jnp.sum(proj * log_probs, axis=0, keepdims=True)
    grad = wgt_ref[...] * (probs * jnp.sum(proj, axis=0, keepdims=True) - proj)
    grad_logits = jnp.concatenate(
        [jnp.where(act == a, grad, 0.0).astype(BF16) for a in range(n_act)], axis=0
    )
    grad_hidden = dot(w2_ref[...], grad_logits, 0, 0)
    grad_pre = jnp.where(pre > 0.0, grad_hidden, 0.0).astype(BF16)
    gp_ref[...] = grad_pre
    ones = jnp.ones((8, cols), BF16)

    @pl.when(step == 0)
    def _():
        acc_ref[...] = jnp.zeros_like(acc_ref)
        gb1_ref[...] = jnp.zeros_like(gb1_ref)
        gb2_ref[...] = jnp.zeros_like(gb2_ref)

    acc_ref[...] += dot(grad_logits, hidden, 1, 1)
    gb1_ref[...] += dot(ones, grad_pre, 1, 1)
    gb2_ref[...] += dot(ones, grad_logits, 1, 1)

    @pl.when(step == last)
    def _():
        used = n_act * n_atom
        if gw2_ref.shape[0] > used:
            gw2_ref[used:, :] = jnp.zeros((gw2_ref.shape[0] - used, gw2_ref.shape[1]), F32)
        for a in range(n_act):
            gw2_ref[a * n_atom:(a + 1) * n_atom, :] = acc_ref[a * slot:a * slot + n_atom, :]


def head(pre, w2p, b2p, act, tp, nxt, low, frac, wgt, n_act, n_atom, slot):
    hid, rows = pre.shape
    tile = 256 if rows % 256 == 0 else rows
    wide = n_act * slot
    packed = pad_up(n_act * n_atom, 8)
    lanes = lambda height: pl.BlockSpec((height, tile), lambda i: (0, i))
    whole = lambda shape: pl.BlockSpec(shape, lambda i: (0,) * len(shape))
    return pl.pallas_call(
        functools.partial(head_kernel, n_act, n_atom, slot),
        grid=(rows // tile,),
        in_specs=[
            lanes(hid), whole((wide, hid)), whole((wide, 1)), lanes(1),
            pl.BlockSpec((n_act, n_atom, tile), lambda i: (0, 0, i)),
            lanes(1), lanes(n_atom), lanes(n_atom), lanes(1),
        ],
        out_specs=[lanes(hid), whole((packed, hid)), whole((8, hid)), whole((8, wide)), lanes(1)],
        out_shape=[
            jax.ShapeDtypeStruct((hid, rows), BF16),
            jax.ShapeDtypeStruct((packed, hid), F32),
            jax.ShapeDtypeStruct((8, hid), F32),
            jax.ShapeDtypeStruct((8, wide), F32),
            jax.ShapeDtypeStruct((1, rows), F32),
        ],
        scratch_shapes=[pltpu.VMEM((wide, hid), F32)],
        compiler_params=pltpu.CompilerParams(vmem_limit_bytes=VMEM_LIMIT),
        name="head",
    )(pre, w2p, b2p, act, tp, nxt, low, frac, wgt)


def plan(n_dev, used):
    bits = n_dev.bit_length() - 1
    unit = 8 * n_dev
    units = -(-used // unit)
    rest = list(range(1, bits))
    head_bits, tail_bits = rest[:3], rest[3:]
    orders = []
    for turn in range(max(1, len(head_bits))):
        orders.append([0] + head_bits[turn:] + head_bits[:turn] + tail_bits)
    light = len(orders) - 1
    names = [(s, o) for s in range(2) for o in range(len(orders))]
    give = [k for k in names if k[1] != light] + [k for k in names if k[1] == light]
    share = {k: 0 for k in names}
    for u in range(units):
        share[give[u % len(give)]] += 1
    parts, base = [], 0
    for k in names:
        if share[k]:
            parts.append((base, share[k] * unit, orders[k[1]]))
            base += share[k] * unit
    return parts, base


def chunk_of(rows):
    best = 8
    for c in range(8, 65, 8):
        if rows % c == 0:
            best = c
    return best


def sum_kernel(
    parts, bits, feat_ref, gp_ref, w2_ref, tail_ref, o1_ref, o2_ref, o3_ref,
    mine, heard, total, send_sem, recv_sem, out_sem,
):
    me = lax.axis_index("dp")
    n_feat = feat_ref.shape[0]
    n_w2 = w2_ref.shape[0]
    n_tail = tail_ref.shape[0]
    sections = ((0, n_feat, o1_ref), (n_feat, n_w2, o2_ref), (n_feat + n_w2, n_tail, o3_ref))

    def bit_of(b):
        return lax.rem(lax.div(me, 1 << b), 2)

    def partner(b):
        return me + (1 << b) - 2 * (1 << b) * bit_of(b)

    barrier = pltpu.get_barrier_semaphore()
    for b in range(bits):
        pl.semaphore_signal(barrier, inc=1, device_id=(partner(b),), device_id_type=MESH)
    pl.semaphore_wait(barrier, bits)

    def rows_at(offset, count):
        return pl.ds(pl.multiple_of(offset, 8), count)

    spans = []
    for base, length, order in parts:
        offs, off, here = [], base, length
        heard_at = base
        for b in order:
            half = here // 2
            keep = off + bit_of(b) * half
            away = off + (1 - bit_of(b)) * half
            offs.append((keep, away, half, heard_at))
            heard_at += half
            off, here = keep, half
        spans.append(offs)

    def scatter(p, i):
        keep, away, half, heard_at = spans[p][i]
        return pltpu.make_async_remote_copy(
            src_ref=mine.at[rows_at(away, half)],
            dst_ref=heard.at[pl.ds(heard_at, half)],
            send_sem=send_sem.at[p, i],
            recv_sem=recv_sem.at[p, i],
            device_id=(partner(parts[p][2][i]),),
            device_id_type=MESH,
        )

    def gather(p, i):
        keep, away, half, heard_at = spans[p][i]
        return pltpu.make_async_remote_copy(
            src_ref=total.at[rows_at(keep, half)],
            dst_ref=total.at[rows_at(keep, half)],
            send_sem=send_sem.at[p, bits + i],
            recv_sem=recv_sem.at[p, bits + i],
            device_id=(partner(parts[p][2][i]),),
            device_id_type=MESH,
        )

    for p, (base, length, order) in enumerate(parts):
        stop = base + length
        end = min(stop, n_feat)
        if end > base:
            full = (end - base) // 256

            @pl.loop(0, full)
            def _(k, base=base):
                at = rows_at(base + k * 256, 256)
                mine[at, :] = dot(feat_ref[at, :], gp_ref[...], 1, 1)

            left = base + full * 256
            if left < end:
                mine[left:end, :] = dot(feat_ref[left:end, :], gp_ref[...], 1, 1)
        for start, count, src in ((n_feat, n_w2, w2_ref), (n_feat + n_w2, n_tail, tail_ref)):
            lo, hi = max(base, start), min(stop, start + count)
            if hi > lo:
                mine[lo:hi, :] = src[lo - start:hi - start, :]
        scatter(p, 0).start()

    for i in range(bits):
        for p in range(len(parts)):
            scatter(p, i).wait_recv()
            keep, away, half, heard_at = spans[p][i]
            chunk = chunk_of(half)
            into = mine if i < bits - 1 else total

            @pl.loop(0, half // chunk)
            def _(k, keep=keep, heard_at=heard_at, chunk=chunk, into=into):
                at = rows_at(keep + k * chunk, chunk)
                into[at, :] = mine[at, :] + heard[rows_at(heard_at + k * chunk, chunk), :]

            if i < bits - 1:
                scatter(p, i + 1).start()
            else:
                gather(p, i).start()

    for i in range(bits - 1, -1, -1):
        for p in range(len(parts)):
            gather(p, i).wait_recv()
            if i > 0:
                gather(p, i - 1).start()

    copies = []
    for p, (base, length, order) in enumerate(parts):
        for s, (start, count, out) in enumerate(sections):
            lo, hi = max(base, start), min(base + length, start + count)
            if hi > lo:
                copy = pltpu.make_async_copy(
                    total.at[pl.ds(lo, hi - lo)], out.at[pl.ds(lo - start, hi - lo)], out_sem.at[p, s]
                )
                copy.start()
                copies.append(copy)
    for p in range(len(parts)):
        for i in range(bits):
            scatter(p, i).wait_send()
            gather(p, i).wait_send()
    for copy in copies:
        copy.wait()


def sum_over(n_dev, feat, gp, gw2, small):
    n_feat = feat.shape[0]
    hid = gp.shape[0]
    parts, height = plan(n_dev, n_feat + gw2.shape[0] + small.shape[0])
    room = height - n_feat - gw2.shape[0]
    small = jnp.pad(small, ((0, room - small.shape[0]), (0, 0)))
    bits = n_dev.bit_length() - 1
    whole = pl.BlockSpec(memory_space=pltpu.VMEM)
    anywhere = pl.BlockSpec(memory_space=pl.ANY)
    return pl.pallas_call(
        functools.partial(sum_kernel, parts, bits),
        in_specs=[whole] * 4,
        out_specs=[anywhere] * 3,
        out_shape=[
            jax.ShapeDtypeStruct((n_feat, hid), F32),
            jax.ShapeDtypeStruct(gw2.shape, F32),
            jax.ShapeDtypeStruct(small.shape, F32),
        ],
        scratch_shapes=[
            pltpu.VMEM((height, hid), F32),
            pltpu.VMEM((height, hid), F32),
            pltpu.VMEM((height, hid), F32),
            pltpu.SemaphoreType.DMA((len(parts), 2 * bits)),
            pltpu.SemaphoreType.DMA((len(parts), 2 * bits)),
            pltpu.SemaphoreType.DMA((len(parts), 3)),
        ],
        compiler_params=pltpu.CompilerParams(
            collective_id=0, has_side_effects=True, vmem_limit_bytes=VMEM_LIMIT
        ),
        name="sum_over_devices",
    )(feat, gp, gw2, small)


def on_device(
    n_dev, features, w_one, b_one, w_two, b_two, action, target_probs, next_action, lower_idx, upper_frac, is_weight,
):
    rows = features.shape[0]
    hid = w_one.shape[0]
    n_act, n_atom = target_probs.shape[1:]
    slot = pad_up(n_atom, 16)
    wide = n_act * slot
    feat = features.T
    pre = dot(w_one, features, 1, 1) + b_one[:, None]
    w2p = jnp.pad(w_two.T.reshape(n_act, n_atom, hid), ((0, 0), (0, slot - n_atom), (0, 0))).reshape(wide, hid)
    b2p = jnp.pad(b_two.reshape(n_act, n_atom), ((0, 0), (0, slot - n_atom))).reshape(wide, 1)
    gp, gw2, gb1, gb2, ce = head(
        pre, w2p, b2p, action[None, :], target_probs.transpose(1, 2, 0), next_action[None, :],
        lower_idx.T, upper_frac.T, is_weight[None, :], n_act, n_atom, slot,
    )
    ce = ce[0]
    tops = jnp.where(jnp.arange(hid) == lax.axis_index("dp"), jnp.max(ce), 0.0)
    loss = jnp.where(jnp.arange(hid) == 0, jnp.sum(is_weight * ce), 0.0)
    b2_rows = -(-wide // hid)
    b2_flat = jnp.pad(gb2[0], (0, b2_rows * hid - wide)).reshape(b2_rows, hid)
    small = jnp.concatenate([gb1[:1], tops[None], loss[None], b2_flat], axis=0)
    g1, g2, rest = sum_over(n_dev, feat, gp, gw2, small)
    top = jnp.max(jnp.where(jnp.arange(hid) < n_dev, rest[1], -jnp.inf))
    grad_b2 = rest[3:3 + b2_rows].reshape(-1)[:wide].reshape(n_act, slot)[:, :n_atom].reshape(-1)
    mean_loss = rest[2, 0] / (rows * n_dev)
    priorities = ce / jnp.maximum(top, 1.0)
    return g1.T, rest[0], g2[:n_act * n_atom].T, grad_b2, mean_loss, priorities


def solution(mesh):
    in_specs = (
        P("dp", None), P(), P(), P(), P(), P("dp"), P("dp", None, None), P("dp"),
        P("dp", None), P("dp", None), P("dp"),
    )
    out_specs = (P(), P(), P(), P(), P(), P("dp"))
    return jax.shard_map(
        functools.partial(on_device, mesh.shape["dp"]),
        mesh=mesh, in_specs=in_specs, out_specs=out_specs, check_vma=False,
    )
```

time: 284 us -> 155 us (0.55)
  Pallas kernels: 0 us -> 116 us
  waiting for transfers between devices: 94.3 us -> 0 us
  blocking collectives: 84.6 us -> 0 us
  local copies, waits for them, and re-layouts: 51.4 us -> 21.2 us
  matrix products: 23.4 us -> 7.85 us
  between operations: 16.7 us -> 3.15 us
  other arithmetic: 12.5 us -> 5.74 us
    pallas_call x0 -> x2, Pallas kernels: none -> 116 us  [the longest x1 100 us: sum_over(): pl.pallas_call(functools.partial(sum_kernel, parts, bits), in_specs=[whol...]
    psum x1 -> x0, waiting for transfers between devices: 94.3 us -> none  [on_device(): grad_w1 = lax.psum(local_w1, 'dp')]
    pmax x1 -> x0, blocking collectives: 43.3 us -> none  [on_device(): top = lax.pmax(local_top, 'dp')]
    psum x1 -> x0, blocking collectives: 41.3 us -> none  [on_device(): grad_b1, grad_w2, grad_b2 = lax.psum((local_b1, local_w2, local_b2), 'dp')]
    gather x3 -> x0, local copies, waits for them, and re-layouts: 21.3 us -> none  [the longest x2 10.8 us: forward_loss(): jnp.take_along_axis(target_probs, next_action[:, None, None], axis=1)]
    dot_general x5 -> x1, matrix products: 23.4 us -> 7.85 us  [dot(): lax.dot_general(a, b, (((ca,), (cb,)), ((), ())), preferred_element_type=...]
    unnamed x27 -> x11, local copies, waits for them, and re-layouts: 16.6 us -> 6.32 us
    reshape x2 -> x5, local copies, waits for them, and re-layouts: 11.3 us -> 4.68 us  [the longest x1 2.52 us: on_device(): w_two.T.reshape(n_act, n_atom, hid)]
  transfers between devices with their start and end apart: 1 -> 0, of which waited for: 1 -> 0; matrix products, arithmetic and copies ran while one was open for 1% -> 0% of each run, Pallas kernels for 0% -> 0%
where the time goes in v1:
time: 155 us; the launch traced here: 154 us
  Pallas kernels  116 us (75%)
  local copies, waits for them, and re-layouts  21.2 us (14%)
  matrix products  7.85 us (5%)
  other arithmetic  5.74 us (4%)
  between operations  3.15 us (2%)
    pallas_call x1, Pallas kernels, sum_over(): pl.pallas_call(functools.partial(sum_kernel, parts, bits), in_specs=[whol...  100 us
    pallas_call x1, Pallas kernels, head(): pl.pallas_call(functools.partial(head_kernel, n_act, n_atom, slot), grid=...  16.2 us
    dot_general x1, matrix products, dot(): lax.dot_general(a, b, (((ca,), (cb,)), ((), ())), preferred_element_type=...  7.85 us
    unnamed x11, local copies, waits for them, and re-layouts  6.32 us

profile of v1, /device:TPU:1, one launch (start us, length us, event | category | flops | bytes accessed | tf_op | source)
XLA Modules:
  0.0 154.3 jit_solution(5034408665943605966)
XLA Ops:
  0.6 0.0 copy-start
  0.7 2.5 %reshape.57 = bf16[18,51,512]{2,1,0:T(8,128)(2,1)} reshape(bf16[918,512]{1,0:T(8,128)(2,1)} %bitcast.23) | data formatting | bytes 1880064 | tf_op jit(solution)/shard_map/reshape | solution.py:312
  3.2 2.4 %pad.16 = bf16[18,64,512]{2,1,0:T(8,128)(2,1)} pad(bf16[18,51,512]{2,1,0:T(8,128)(2,1)} %reshape.57, bf16[]{:T(256)} %constant.8.clone.1), padding=0_0x0_13x0_0 | pad | bytes 2119682 | tf_op jit(solution)/shard_map/jit(_pad)/pad | solution.py:312
  5.5 0.0 copy-done
  5.5 7.8 %convolution_add_fusion.pre_ref = f32[512,1024]{1,0:T(8,128)} fusion(bf16[512,3136]{0,1:T(8,128)(2,1)S(1)} %copy-done, bf16[1024,3136]{0,1:T(8,128)(2,1)} %param.11, f32[512]{0:T(512)S(1)} %copy-done.4), kind=kOutput, calls=%fused_computation.1 | convolution fusion | flops 3288858624 | bytes 11732992 | tf_op jit(solution)/shard_map/dot_general | solution.py:21
  13.4 0.1 reshape.59
  13.5 1.4 reshape.63.b2_ref
  14.9 16.2 %head.1 = (bf16[512,1024]{1,0:T(8,128)(2,1)}, f32[920,512]{1,0:T(8,128)}, f32[8,512]{1,0:T(8,128)}, f32[8,1152]{1,0:T(8,128)}, f32[1,1024]{1,0:T(1,128)}) custom-call(f32[512,1024]{1,0:T(8,128)} %convolution_add_fusion.pre_ref, bf16[1152,512]{1,0:T(8,128)(2,1)} %bitcast.21, f32[1152,1]{1,0:T(8,128)} %reshape.63.b2_ref, s32[1,1024]{1,0:T(1,128)} %bitcast.31, ...), custom_call_target="tpu_custom_call" | custom-call | tf_op jit(solution)/shard_map/head/pallas_call | solution.py:96
  31.1 1.3 multiply_reduce_fusion
  32.4 1.3 reduce_max.18
  33.7 1.3 compare_select_fusion
  35.0 0.8 slice_reduce_fusion
  35.8 0.7 slice.29
  36.5 0.7 select_maximum_fusion.tail_ref
  37.2 100.2 %sum_over_devices.1 = (f32[3136,512]{1,0:T(8,128)}, f32[920,512]{1,0:T(8,128)}, f32[40,512]{1,0:T(8,128)}) custom-call(bf16[3136,1024]{1,0:T(8,128)(2,1)} %bitcast.19, bf16[512,1024]{1,0:T(8,128)(2,1)} %get-tuple-element.14.gp_ref, f32[920,512]{1,0:T(8,128)} %get-tuple-element.15.w2_ref, f32[40,512]{1,0:T(8,128)} %select_maximum_fusion.tail_ref), custom_call_target="tpu_custom_call" | custom-call | tf_op jit(solution)/shard_map/sum_over_devices/pallas_call | solution.py:278
  137.4 1.4 fusion
  138.7 0.6 select_reduce_fusion
  140.0 0.6 broadcast_divide_fusion
  140.6 0.7 slice.33
  141.3 0.1 slice.34
  141.4 0.7 reshape.62
  142.1 1.2 slice.36
  143.9 2.9 %slice_bitcast_fusion = f32[512,918]{0,1:T(8,128)} fusion(f32[920,512]{1,0:T(8,128)} %get-tuple-element.21), kind=kLoop, calls=%fused_computation | loop fusion | bytes 3760128 | tf_op jit(solution)/shard_map/transpose | solution.py:329
  146.8 6.3 %copy.19 = f32[512,3136]{0,1:T(8,128)} copy(f32[512,3136]{0,1:T(8,128)} %bitcast.20) | data formatting | bytes 12845056
  (11 shorter events, 0.0 us)
Async XLA Ops:
  0.6 4.9 %copy-start = (bf16[512,3136]{0,1:T(8,128)(2,1)S(1)}, bf16[512,3136]{0,1:T(8,128)(2,1)}, u32[]{:S(2)}) copy-start(bf16[512,3136]{0,1:T(8,128)(2,1)} %param.12) | copy-start | bytes 9633796
  0.6 4.9 %copy-start.4 = (f32[512]{0:T(512)S(1)}, f32[512]{0:T(512)}, u32[]{:S(2)}) copy-start(f32[512]{0:T(512)} %param.13) | copy-start | bytes 6148
  5.5 7.9 %copy-start.3 = (f32[918]{0:T(1024)S(1)}, f32[918]{0:T(1024)}, u32[]{:S(2)}) copy-start(f32[918]{0:T(1024)} %param.15) | copy-start | bytes 11020
  14.9 16.2 %copy-start.2 = (f32[1024]{0:T(1024)S(1)}, f32[1024]{0:T(1024)}, u32[]{:S(2)}) copy-start(f32[1024]{0:T(1024)} %param.21) | copy-start | bytes 12292
  37.2 102.8 %copy-start.1 = (f32[1,1024]{1,0:T(1,128)S(1)}, f32[1,1024]{1,0:T(1,128)}, u32[]{:S(2)}) copy-start(f32[1,1024]{1,0:T(1,128)} %get-tuple-element.17) | copy-start | bytes 12292

commit v2 on v1

--- a/solution.py
+++ b/solution.py
@@ -10,7 +10,9 @@
 MESH = pl.DeviceIdType.MESH
 F32 = jnp.float32
 BF16 = jnp.bfloat16
-VMEM_LIMIT = 60 * 1024 * 1024
+HEAD_LIMIT = 60 * 1024 * 1024
+SUM_LIMIT = 40 * 1024 * 1024
+SETS = 3
 
 
 def pad_up(value, step):
@@ -24,19 +26,29 @@
 def head_kernel(
     n_act, n_atom, slot,
     pre_ref, w2_ref, b2_ref, act_ref, tp_ref, nxt_ref, low_ref, frac_ref, wgt_ref,
-    gp_ref, gw2_ref, gb1_ref, gb2_ref, ce_ref, acc_ref,
+    gp_ref, gw2_ref, gb1_ref, gb2_ref, ce_ref, acc_ref, w2p_ref, b2t_ref,
 ):
     step = pl.program_id(0)
     last = pl.num_programs(0) - 1
+
+    @pl.when(step == 0)
+    def _():
+        w2p_ref[...] = jnp.zeros_like(w2p_ref)
+        b2t_ref[...] = jnp.zeros_like(b2t_ref)
+        b2t_ref[0:n_atom, 0:n_act] = b2_ref[...].T
+        for a in range(n_act):
+            w2p_ref[a * slot:a * slot + n_atom, :] = w2_ref[a * n_atom:(a + 1) * n_atom, :]
+
     pre = pre_ref[...]
     cols = pre.shape[1]
     hidden = jnp.maximum(pre, 0.0).astype(BF16)
-    logits = dot(w2_ref[...], hidden, 1, 0) + b2_ref[...]
+    logits = dot(w2p_ref[...], hidden, 1, 0)
+    bias = b2t_ref[...]
     act = act_ref[...]
     nxt = nxt_ref[...]
     chosen = jnp.zeros((slot, cols), F32)
     for a in range(n_act):
-        chosen = jnp.where(act == a, logits[a * slot:(a + 1) * slot], chosen)
+        chosen = jnp.where(act == a, logits[a * slot:(a + 1) * slot] + bias[:, a:a + 1], chosen)
     atom = lax.broadcasted_iota(jnp.int32, (slot, cols), 0)
     real = atom < n_atom
     chosen = jnp.where(real, chosen, -jnp.inf)
@@ -62,7 +74,7 @@
     grad_logits = jnp.concatenate(
         [jnp.where(act == a, grad, 0.0).astype(BF16) for a in range(n_act)], axis=0
     )
-    grad_hidden = dot(w2_ref[...], grad_logits, 0, 0)
+    grad_hidden = dot(w2p_ref[...], grad_logits, 0, 0)
     grad_pre = jnp.where(pre > 0.0, grad_hidden, 0.0).astype(BF16)
     gp_ref[...] = grad_pre
     ones = jnp.ones((8, cols), BF16)
@@ -86,7 +98,7 @@
             gw2_ref[a * n_atom:(a + 1) * n_atom, :] = acc_ref[a * slot:a * slot + n_atom, :]
 
 
-def head(pre, w2p, b2p, act, tp, nxt, low, frac, wgt, n_act, n_atom, slot):
+def head(pre, w2, b2, act, tp, nxt, low, frac, wgt, n_act, n_atom, slot):
     hid, rows = pre.shape
     tile = 256 if rows % 256 == 0 else rows
     wide = n_act * slot
@@ -97,7 +109,7 @@
         functools.partial(head_kernel, n_act, n_atom, slot),
         grid=(rows // tile,),
         in_specs=[
-            lanes(hid), whole((wide, hid)), whole((wide, 1)), lanes(1),
+            lanes(hid), whole(w2.shape), whole(b2.shape), lanes(1),
             pl.BlockSpec((n_act, n_atom, tile), lambda i: (0, 0, i)),
             lanes(1), lanes(n_atom), lanes(n_atom), lanes(1),
         ],
@@ -109,10 +121,14 @@
             jax.ShapeDtypeStruct((8, wide), F32),
             jax.ShapeDtypeStruct((1, rows), F32),
         ],
-        scratch_shapes=[pltpu.VMEM((wide, hid), F32)],
-        compiler_params=pltpu.CompilerParams(vmem_limit_bytes=VMEM_LIMIT),
+        scratch_shapes=[
+            pltpu.VMEM((wide, hid), F32),
+            pltpu.VMEM((wide, hid), BF16),
+            pltpu.VMEM((slot, pad_up(n_act, 128)), F32),
+        ],
+        compiler_params=pltpu.CompilerParams(vmem_limit_bytes=HEAD_LIMIT),
         name="head",
-    )(pre, w2p, b2p, act, tp, nxt, low, frac, wgt)
+    )(pre, w2, b2, act, tp, nxt, low, frac, wgt)
 
 
 def plan(n_dev, used):
@@ -125,7 +141,7 @@
     for turn in range(max(1, len(head_bits))):
         orders.append([0] + head_bits[turn:] + head_bits[:turn] + tail_bits)
     light = len(orders) - 1
-    names = [(s, o) for s in range(2) for o in range(len(orders))]
+    names = [(s, o) for s in range(SETS) for o in range(len(orders))]
     give = [k for k in names if k[1] != light] + [k for k in names if k[1] == light]
     share = {k: 0 for k in names}
     for u in range(units):
@@ -147,13 +163,26 @@
 
 
 def sum_kernel(
-    parts, bits, feat_ref, gp_ref, w2_ref, tail_ref, o1_ref, o2_ref, o3_ref,
-    mine, heard, total, send_sem, recv_sem, out_sem,
+    parts, bits, feat_hbm, gp_ref, w2_ref, gb1_ref, gb2_ref, ce_ref, wgt_ref,
+    o1_ref, o2_ref, o3_ref, prio_ref,
+    mine, heard, total, feat_ref, send_sem, recv_sem, out_sem, in_sem,
 ):
     me = lax.axis_index("dp")
     n_feat = feat_ref.shape[0]
     n_w2 = w2_ref.shape[0]
-    n_tail = tail_ref.shape[0]
+    n_tail = o3_ref.shape[0]
+    hid = gp_ref.shape[0]
+    tail_at = n_feat + n_w2
+
+    loads = []
+    for p, (base, length, order) in enumerate(parts):
+        end = min(base + length, n_feat)
+        if end > base:
+            at = pl.ds(base, end - base)
+            loads.append(pltpu.make_async_copy(feat_hbm.at[at], feat_ref.at[at], in_sem.at[p]))
+            loads[-1].start()
+        else:
+            loads.append(None)
     sections = ((0, n_feat, o1_ref), (n_feat, n_w2, o2_ref), (n_feat + n_w2, n_tail, o3_ref))
 
     def bit_of(b):
@@ -209,6 +238,7 @@
         stop = base + length
         end = min(stop, n_feat)
         if end > base:
+            loads[p].wait()
             full = (end - base) // 256
 
             @pl.loop(0, full)
@@ -219,10 +249,24 @@
             left = base + full * 256
             if left < end:
                 mine[left:end, :] = dot(feat_ref[left:end, :], gp_ref[...], 1, 1)
-        for start, count, src in ((n_feat, n_w2, w2_ref), (n_feat + n_w2, n_tail, tail_ref)):
-            lo, hi = max(base, start), min(stop, start + count)
-            if hi > lo:
-                mine[lo:hi, :] = src[lo - start:hi - start, :]
+        lo, hi = max(base, n_feat), min(stop, tail_at)
+        if hi > lo:
+            mine[lo:hi, :] = w2_ref[lo - n_feat:hi - n_feat, :]
+        lo, hi = max(base, tail_at), stop
+        if hi > lo:
+            mine[lo:hi, :] = jnp.zeros((hi - lo, hid), F32)
+            ce = ce_ref[...]
+            lane = lax.broadcasted_iota(jnp.int32, (1, hid), 1)
+            rows = [
+                gb1_ref[0:1, :],
+                jnp.where(lane == me, jnp.max(ce, axis=1, keepdims=True), 0.0),
+                jnp.where(lane == 0, jnp.sum(ce * wgt_ref[...], axis=1, keepdims=True), 0.0),
+            ]
+            for at in range(0, gb2_ref.shape[1], hid):
+                rows.append(gb2_ref[0:1, at:min(at + hid, gb2_ref.shape[1])])
+            for r, row in enumerate(rows):
+                if lo <= tail_at + r < hi:
+                    mine[tail_at + r:tail_at + r + 1, 0:row.shape[1]] = row
         scatter(p, 0).start()
 
     for i in range(bits):
@@ -242,22 +286,24 @@
             else:
                 gather(p, i).start()
 
+    copies = []
     for i in range(bits - 1, -1, -1):
-        for p in range(len(parts)):
+        for p, (base, length, order) in enumerate(parts):
             gather(p, i).wait_recv()
             if i > 0:
                 gather(p, i - 1).start()
-
-    copies = []
-    for p, (base, length, order) in enumerate(parts):
-        for s, (start, count, out) in enumerate(sections):
-            lo, hi = max(base, start), min(base + length, start + count)
-            if hi > lo:
-                copy = pltpu.make_async_copy(
-                    total.at[pl.ds(lo, hi - lo)], out.at[pl.ds(lo - start, hi - lo)], out_sem.at[p, s]
-                )
-                copy.start()
-                copies.append(copy)
+                continue
+            for s, (start, count, out) in enumerate(sections):
+                lo, hi = max(base, start), min(base + length, start + count)
+                if hi > lo:
+                    copies.append(pltpu.make_async_copy(
+                        total.at[pl.ds(lo, hi - lo)], out.at[pl.ds(lo - start, hi - lo)], out_sem.at[p, s]
+                    ))
+                    copies[-1].start()
+
+    lane = lax.broadcasted_iota(jnp.int32, (1, hid), 1)
+    tops = jnp.where(lane < (1 << bits), total[tail_at + 1:tail_at + 2, :], -jnp.inf)
+    prio_ref[...] = ce_ref[...] / jnp.maximum(jnp.max(tops, axis=1, keepdims=True), 1.0)
     for p in range(len(parts)):
         for i in range(bits):
             scatter(p, i).wait_send()
@@ -266,37 +312,39 @@
         copy.wait()
 
 
-def sum_over(n_dev, feat, gp, gw2, small):
+def sum_over(n_dev, feat, gp, gw2, gb1, gb2, ce, wgt):
     n_feat = feat.shape[0]
     hid = gp.shape[0]
-    parts, height = plan(n_dev, n_feat + gw2.shape[0] + small.shape[0])
+    parts, height = plan(n_dev, n_feat + gw2.shape[0] + 3 - (-gb2.shape[1] // hid))
     room = height - n_feat - gw2.shape[0]
-    small = jnp.pad(small, ((0, room - small.shape[0]), (0, 0)))
     bits = n_dev.bit_length() - 1
     whole = pl.BlockSpec(memory_space=pltpu.VMEM)
     anywhere = pl.BlockSpec(memory_space=pl.ANY)
     return pl.pallas_call(
         functools.partial(sum_kernel, parts, bits),
-        in_specs=[whole] * 4,
-        out_specs=[anywhere] * 3,
+        in_specs=[anywhere] + [whole] * 6,
+        out_specs=[anywhere] * 3 + [whole],
         out_shape=[
             jax.ShapeDtypeStruct((n_feat, hid), F32),
             jax.ShapeDtypeStruct(gw2.shape, F32),
-            jax.ShapeDtypeStruct(small.shape, F32),
+            jax.ShapeDtypeStruct((room, hid), F32),
+            jax.ShapeDtypeStruct(ce.shape, F32),
         ],
         scratch_shapes=[
             pltpu.VMEM((height, hid), F32),
             pltpu.VMEM((height, hid), F32),
             pltpu.VMEM((height, hid), F32),
+            pltpu.VMEM(feat.shape, feat.dtype),
             pltpu.SemaphoreType.DMA((len(parts), 2 * bits)),
             pltpu.SemaphoreType.DMA((len(parts), 2 * bits)),
             pltpu.SemaphoreType.DMA((len(parts), 3)),
+            pltpu.SemaphoreType.DMA((len(parts),)),
         ],
         compiler_params=pltpu.CompilerParams(
-            collective_id=0, has_side_effects=True, vmem_limit_bytes=VMEM_LIMIT
+            collective_id=0, has_side_effects=True, vmem_limit_bytes=SUM_LIMIT
         ),
         name="sum_over_devices",
-    )(feat, gp, gw2, small)
+    )(feat, gp, gw2, gb1, gb2, ce, wgt)
 
 
 def on_device(
@@ -309,24 +357,15 @@
     wide = n_act * slot
     feat = features.T
     pre = dot(w_one, features, 1, 1) + b_one[:, None]
-    w2p = jnp.pad(w_two.T.reshape(n_act, n_atom, hid), ((0, 0), (0, slot - n_atom), (0, 0))).reshape(wide, hid)
-    b2p = jnp.pad(b_two.reshape(n_act, n_atom), ((0, 0), (0, slot - n_atom))).reshape(wide, 1)
     gp, gw2, gb1, gb2, ce = head(
-        pre, w2p, b2p, action[None, :], target_probs.transpose(1, 2, 0), next_action[None, :],
-        lower_idx.T, upper_frac.T, is_weight[None, :], n_act, n_atom, slot,
+        pre, w_two.T, b_two.reshape(n_act, n_atom), action[None, :], target_probs.transpose(1, 2, 0),
+        next_action[None, :], lower_idx.T, upper_frac.T, is_weight[None, :], n_act, n_atom, slot,
     )
-    ce = ce[0]
-    tops = jnp.where(jnp.arange(hid) == lax.axis_index("dp"), jnp.max(ce), 0.0)
-    loss = jnp.where(jnp.arange(hid) == 0, jnp.sum(is_weight * ce), 0.0)
+    g1, g2, rest, priorities = sum_over(n_dev, feat, gp, gw2, gb1, gb2, ce, is_weight[None, :])
     b2_rows = -(-wide // hid)
-    b2_flat = jnp.pad(gb2[0], (0, b2_rows * hid - wide)).reshape(b2_rows, hid)
-    small = jnp.concatenate([gb1[:1], tops[None], loss[None], b2_flat], axis=0)
-    g1, g2, rest = sum_over(n_dev, feat, gp, gw2, small)
-    top = jnp.max(jnp.where(jnp.arange(hid) < n_dev, rest[1], -jnp.inf))
     grad_b2 = rest[3:3 + b2_rows].reshape(-1)[:wide].reshape(n_act, slot)[:, :n_atom].reshape(-1)
     mean_loss = rest[2, 0] / (rows * n_dev)
-    priorities = ce / jnp.maximum(top, 1.0)
-    return g1.T, rest[0], g2[:n_act * n_atom].T, grad_b2, mean_loss, priorities
+    return g1.T, rest[0], g2[:n_act * n_atom].T, grad_b2, mean_loss, priorities[0]
 
 
 def solution(mesh):

time: 155 us -> 143 us (0.923)
  Pallas kernels: 116 us -> 109 us
  other arithmetic: 5.74 us -> 0 us
  local copies, waits for them, and re-layouts: 21.2 us -> 23.1 us
    unnamed x11 -> x22, local copies, waits for them, and re-layouts: 6.32 us -> 17.7 us
    pallas_call x1, Pallas kernels: 100 us -> 92.8 us  [sum_over(): pl.pallas_call(functools.partial(sum_kernel, parts, bits), in_specs=[anyw...]
    reshape x3 -> x0, local copies, waits for them, and re-layouts: 3.92 us -> none  [the longest x1 2.52 us: on_device(): w_two.T.reshape(n_act, n_atom, hid)]
    pad x3 -> x0, local copies, waits for them, and re-layouts: 2.37 us -> none  [the longest x1 2.36 us: on_device(): jnp.pad(w_two.T.reshape(n_act, n_atom, hid), ((0, 0), (0, slot - n_atom),...]
    slice x3 -> x1, local copies, waits for them, and re-layouts: 2.88 us -> 0.58 us  [on_device(): rest[0]]
    reduce_max x2 -> x0, other arithmetic: 1.9 us -> none  [the longest x1 1.3 us: on_device(): tops = jnp.where(jnp.arange(hid) == lax.axis_index('dp'), jnp.max(ce), 0.0)]
where the time goes in v2:
time: 143 us; the launch traced here: 142 us
  Pallas kernels  109 us (76%)
  local copies, waits for them, and re-layouts  23.1 us (16%)
  matrix products  7.85 us (5%)
  between operations  2.47 us (2%)
    pallas_call x1, Pallas kernels, sum_over(): pl.pallas_call(functools.partial(sum_kernel, parts, bits), in_specs=[anyw...  92.8 us
    unnamed x22, local copies, waits for them, and re-layouts  17.7 us
    pallas_call x1, Pallas kernels, head(): pl.pallas_call(functools.partial(head_kernel, n_act, n_atom, slot), grid=...  16.1 us
    dot_general x1, matrix products, dot(): lax.dot_general(a, b, (((ca,), (cb,)), ((), ())), preferred_element_type=...  7.85 us
    transpose x1, local copies, waits for them, and re-layouts, on_device(): g2[:n_act * n_atom]  2.91 us

profile of v2, /device:TPU:1, one launch (start us, length us, event | category | flops | bytes accessed | tf_op | source)
XLA Modules:
  0.0 142.4 jit_solution(3602834116672580055)
XLA Ops:
  0.6 0.0 copy-start
  0.6 1.9 %copy-done = bf16[512,3136]{0,1:T(8,128)(2,1)S(1)} copy-done((bf16[512,3136]{0,1:T(8,128)(2,1)S(1)}, bf16[512,3136]{0,1:T(8,128)(2,1)}, u32[]{:S(2)}) %copy-start) | copy-done | bytes 3211288
  2.5 7.8 %convolution_add_fusion.pre_ref = f32[512,1024]{1,0:T(8,128)} fusion(bf16[512,3136]{0,1:T(8,128)(2,1)S(1)} %copy-done, bf16[1024,3136]{0,1:T(8,128)(2,1)} %param.11, f32[512]{0:T(512)} %param.13), kind=kOutput, calls=%fused_computation.1 | convolution fusion | flops 3288858624 | bytes 11732992 | tf_op jit(solution)/shard_map/dot_general | solution.py:23
  10.4 0.0 copy-done.9
  10.4 0.7 reshape.25.b2_ref
  11.1 16.1 %head.1 = (bf16[512,1024]{1,0:T(8,128)(2,1)}, f32[920,512]{1,0:T(8,128)}, f32[8,512]{1,0:T(8,128)}, f32[8,1152]{1,0:T(8,128)}, f32[1,1024]{1,0:T(1,128)}) custom-call(f32[512,1024]{1,0:T(8,128)} %convolution_add_fusion.pre_ref, bf16[918,512]{1,0:T(8,128)(2,1)} %bitcast.23, f32[18,51]{1,0:T(8,128)} %reshape.25.b2_ref, s32[1,1024]{1,0:T(1,128)} %bitcast.27, ...), custom_call_target="tpu_custom_call" | custom-call | tf_op jit(solution)/shard_map/head/pallas_call | solution.py:108
  27.2 0.0 copy-done.6
  27.2 0.0 copy-start.2
  27.2 1.5 %copy-done.2 = f32[920,512]{1,0:T(8,128)S(1)} copy-done((f32[920,512]{1,0:T(8,128)S(1)}, f32[920,512]{1,0:T(8,128)}, u32[]{:S(2)}) %copy-start.2) | copy-done | bytes 1884184
  28.8 1.2 copy-done.4
  30.0 0.8 copy-done.5
  30.8 0.7 copy-done.7
  31.5 0.7 copy-done.8
  32.2 92.8 %sum_over_devices.1 = (f32[3136,512]{1,0:T(8,128)S(1)}, f32[920,512]{1,0:T(8,128)S(1)}, f32[40,512]{1,0:T(8,128)S(1)}, f32[1,1024]{1,0:T(1,128)S(1)}) custom-call(bf16[3136,1024]{1,0:T(8,128)(2,1)} %bitcast.21, bf16[512,1024]{1,0:T(8,128)(2,1)S(1)} %copy-done.4, f32[920,512]{1,0:T(8,128)S(1)} %copy-done.2, f32[8,512]{1,0:T(8,128)S(1)} %copy-done.7, ...), custom_call_target="tpu_custom_call" | custom-call | tf_op jit(solution)/shard_map/sum_over_devices/pallas_call | solution.py:323
  125.0 0.0 copy-start.1
  125.0 2.7 %copy-done.1 = f32[3136,512]{1,0:T(8,128)} copy-done((f32[3136,512]{1,0:T(8,128)}, f32[3136,512]{1,0:T(8,128)S(1)}, u32[]{:S(2)}) %copy-start.1) | copy-done | bytes 6422552
  127.7 1.2 copy-done.3
  128.9 0.1 slice.23
  129.0 0.7 reshape.26
  129.7 0.6 slice.20
  130.3 0.5 slice.25
  131.4 2.9 %slice_bitcast_fusion = f32[512,918]{0,1:T(8,128)} fusion(f32[920,512]{1,0:T(8,128)} %copy-done.3), kind=kLoop, calls=%fused_computation | loop fusion | bytes 3760128 | tf_op jit(solution)/shard_map/transpose | solution.py:368
  134.3 6.3 %copy.19 = f32[512,3136]{0,1:T(8,128)} copy(f32[512,3136]{0,1:T(8,128)} %bitcast.17) | data formatting | bytes 12845056
  140.6 0.6 copy.20
  (8 shorter events, 0.0 us)
Async XLA Ops:
  0.6 1.9 %copy-start = (bf16[512,3136]{0,1:T(8,128)(2,1)S(1)}, bf16[512,3136]{0,1:T(8,128)(2,1)}, u32[]{:S(2)}) copy-start(bf16[512,3136]{0,1:T(8,128)(2,1)} %param.12) | copy-start | bytes 9633796
  2.5 7.9 %copy-start.9 = (f32[918]{0:T(1024)S(1)}, f32[918]{0:T(1024)}, u32[]{:S(2)}) copy-start(f32[918]{0:T(1024)} %param.15) | copy-start | bytes 11020
  11.1 16.1 %copy-start.6 = (f32[1024]{0:T(1024)S(1)}, f32[1024]{0:T(1024)}, u32[]{:S(2)}) copy-start(f32[1024]{0:T(1024)} %param.21) | copy-start | bytes 12292
  27.2 1.5 %copy-start.2 = (f32[920,512]{1,0:T(8,128)S(1)}, f32[920,512]{1,0:T(8,128)}, u32[]{:S(2)}) copy-start(f32[920,512]{1,0:T(8,128)} %get-tuple-element.16.w2_ref) | copy-start | bytes 5652484
  28.8 1.2 copy-start.4
  30.0 0.8 copy-start.5
  30.8 0.7 copy-start.7
  31.5 0.7 copy-start.8
  125.0 2.7 %copy-start.1 = (f32[3136,512]{1,0:T(8,128)}, f32[3136,512]{1,0:T(8,128)S(1)}, u32[]{:S(2)}) copy-start(f32[3136,512]{1,0:T(8,128)S(1)} %get-tuple-element.20) | copy-start | bytes 19267588
  127.7 1.2 copy-start.3
